TPU v7x, 32 devices: a whole 2x2x4 slice. The times are simulated.
32 devices in a mesh: section: 2 (over core), expert: 16 (over z, y, x).
Axes of the slice: x: 2, y: 2, z: 4, core: 2. Of those that a mesh axis runs over, the one named last changes fastest.
Arguments:
- tokens: bfloat16 [2, 1024, 2048], P(None, 'expert'), may hold values from -6 to 6
- norm_gain: float32 [2, 2048], P('section'), may hold values from 0.5 to 2
- gate_weight: bfloat16 [2, 16, 2048, 768], P('section', 'expert'), may hold values from -0.125 to 0.125
- up_weight: bfloat16 [2, 16, 2048, 768], P('section', 'expert'), may hold values from -0.125 to 0.125
- down_weight: bfloat16 [2, 16, 768, 2048], P('section', 'expert'), may hold values from -0.21875 to 0.21875
- expert_place: int32 [2, 16], P('section'), may hold values from 0 to 15, each once within a row
- expert_ids: int32 [2, 2, 1024, 8], P('section', None, 'expert'), may hold values from 0 to 15, all different within a row; in each aligned block of 64 rows (0 to 63, 64 to 127, ..., all dimensions but the last counted through in order) at most 40 rows name the same one
- route_weights: float32 [2, 2, 1024, 8], P('section', None, 'expert'), may hold values from 0.05 to 0.4
Outputs:
- final_states: bfloat16 [2, 1024, 2048], P(None, 'expert')
Inputs may be any that keep to these rules, and one draw needn't show every extreme that they name: `expert_ids`: each row names 8 different experts. In each aligned block of 64 rows (one device's tokens of one micro-batch in one layer) no expert is named by more than 40 rows, a bound that some block reaches. `expert_place`: each layer's row names every index along expert once.
All inputs are finite; a program needn't handle non-finite values.
Results may differ from a plain program's by a relative error of at most 0.013.
Values may be sent and summed in bfloat16 or wider, within the bound.
A program may use at most 128 MiB of HBM per device.

v0:
```python
import jax
import jax.numpy as jnp
from jax import lax
from jax.sharding import PartitionSpec as P

EPSILON = 1e-06


def from_behind(array, axis, by):
    size = lax.axis_size(axis)
    return lax.ppermute(array, axis, [(i, (i + by) % size) for i in range(size)])


def normalize(values, gain_row):
    widened = values.astype(jnp.float32)
    inverse_rms = lax.rsqrt(jnp.mean(widened * widened, axis=-1, keepdims=True) + EPSILON)
    return (widened * inverse_rms * gain_row[None, :]).astype(jnp.bfloat16)


def expert_ffn(row_block, gate_matrix, up_matrix, down_matrix):
    gate_part = jnp.dot(row_block, gate_matrix, preferred_element_type=jnp.float32)
    up_part = jnp.dot(row_block, up_matrix, preferred_element_type=jnp.float32)
    hidden_units = (jax.nn.silu(gate_part) * up_part).astype(jnp.bfloat16)
    return jnp.dot(hidden_units, down_matrix, preferred_element_type=jnp.float32).astype(
        jnp.bfloat16
    )


def local(
    tokens, norm_gain, gate_weight, up_weight, down_weight, expert_place, expert_ids, route_weights
):
    sections = lax.axis_size("section")
    groups = lax.axis_size("expert")
    section_index = lax.axis_index("section")
    micro_count = tokens.shape[0]
    tok_rows = tokens.shape[1]
    model_width = tokens.shape[2]
    top_count = expert_ids.shape[3]
    experts_all = expert_place.shape[1]
    capacity = max(2, 5 * tok_rows * top_count // (4 * experts_all))
    expert_lanes = jnp.arange(experts_all, dtype=jnp.int32)
    flat_token = jnp.arange(tok_rows * top_count, dtype=jnp.int32) // top_count
    own_params = (
        norm_gain[0],
        gate_weight[0, 0],
        up_weight[0, 0],
        down_weight[0, 0],
        expert_place[0],
        expert_ids[0],
        route_weights[0],
    )

    def run_rows(received, active, params):
        row_shape = received.shape
        flat_rows = received.reshape(-1, model_width)
        computed = lax.cond(
            active,
            lambda row_block: expert_ffn(row_block, params[1], params[2], params[3]),
            lambda row_block: jnp.zeros_like(row_block),
            flat_rows,
        )
        return computed.reshape(row_shape)

    def layer_step(hidden, micro_index, active, params):
        normed = normalize(hidden, params[0])
        holder_table = params[4]
        chosen = lax.dynamic_index_in_dim(params[5], micro_index, 0, keepdims=False).reshape(-1)
        weights = lax.dynamic_index_in_dim(params[6], micro_index, 0, keepdims=False)
        onehot = (chosen[:, None] == expert_lanes[None, :]).astype(jnp.int32)
        before = jnp.cumsum(onehot, axis=0) - onehot
        position = jnp.sum(before * onehot, axis=1)
        holder = jnp.sum(onehot * holder_table[None, :], axis=1)
        target = holder * capacity + position
        outgoing = (
            jnp.zeros((groups * capacity, model_width), jnp.bfloat16)
            .at[target]
            .set(normed[flat_token])
        )
        outgoing = outgoing.reshape(groups, capacity, model_width)
        received = lax.all_to_all(outgoing, "expert", split_axis=0, concat_axis=0, tiled=True)
        returned_rows = lax.all_to_all(
            run_rows(received, active, params), "expert", split_axis=0, concat_axis=0, tiled=True
        )
        picked = returned_rows.reshape(groups * capacity, model_width)[target]
        picked = picked.astype(jnp.float32).reshape(tok_rows, top_count, model_width)
        mixture = jnp.einsum("tk,tkd->td", weights, picked)
        return (hidden.astype(jnp.float32) + mixture).astype(jnp.bfloat16)

    other_mats = from_behind((own_params[1], own_params[2], own_params[3]), "section", 1)
    other_ints = from_behind((own_params[4], own_params[5]), "section", 1)
    other_floats = from_behind((own_params[0], own_params[6]), "section", 1)
    other_params = (
        other_floats[0],
        other_mats[0],
        other_mats[1],
        other_mats[2],
        other_ints[0],
        other_ints[1],
        other_floats[1],
    )
    is_first = section_index == 0
    first_params = tuple(
        (jnp.where(is_first, mine, theirs) for mine, theirs in zip(own_params, other_params))
    )
    second_params = tuple(
        (jnp.where(is_first, theirs, mine) for mine, theirs in zip(own_params, other_params))
    )
    share = micro_count // sections
    always = jnp.array(True)
    micro_index = section_index * share + 0
    hidden = lax.dynamic_index_in_dim(tokens, micro_index, 0, keepdims=False)
    hidden = layer_step(hidden, micro_index, always, first_params)
    hidden = layer_step(hidden, micro_index, always, second_params)
    own_finals = [hidden]
    return lax.all_gather(jnp.stack(own_finals), "section", axis=0, tiled=True)


def solution(mesh):
    in_specs = (
        P(None, "expert", None),
        P("section", None),
        P("section", "expert", None, None),
        P("section", "expert", None, None),
        P("section", "expert", None, None),
        P("section", None),
        P("section", None, "expert", None),
        P("section", None, "expert", None),
    )
    out_specs = P(None, "expert", None)
    return jax.shard_map(local, mesh=mesh, in_specs=in_specs, out_specs=out_specs, check_vma=False)
```

profile of v0, /device:TPU:15, one launch (start us, length us, event | category | flops | bytes accessed | tf_op | source)
XLA Modules:
  0.0 339.1 jit_solution(991331135753815844)
XLA Ops:
  0.0 0.7 collective-permute-start.1
  0.7 0.5 collective-permute-start.3
  1.2 1.1 fusion.32
  2.3 0.7 broadcast_select_fusion.2
  3.0 0.7 dynamic-slice_select_fusion
  3.7 0.1 copy.12
  3.8 0.1 eq.66
  3.9 0.1 eq.62
  4.1 0.1 eq.58
  4.1 0.1 eq.54
  4.3 1.2 reduce-window.16
  5.4 0.2 slice_reduce_fusion
  5.7 1.2 reduce-window.14
  6.8 0.2 slice_reduce_fusion.1
  7.1 0.1 select_reduce_fusion
  7.2 0.1 select_reduce_fusion.1
  7.3 0.7 broadcast_select_fusion
  8.0 1.1 fusion.34
  9.1 22.8 %scatter_custom_fusion = bf16[640,2048]{1,0:T(8,128)(2,1)} fusion(s32[512]{0:T(512)S(1)} %bitcast.129, bf16[64,2048]{1,0:T(8,128)(2,1)S(1)} %fusion.34, s32[1024]{0:T(1024)S(1)} %pad_clamp_fusion.2, bf16[]{:T(256)} %constant.59.clone.1), kind=kCustom, calls=%fused_computation.30 | custom fusion | bytes 2621442 | tf_op jit(solution)/shard_map/scatter | solution.py:77
  31.9 6.6 %all-to-all-start = ((bf16[16,40,2048]{2,1,0:T(8,128)(2,1)}), bf16[16,40,2048]{2,1,0:T(8,128)(2,1)S(1)}, u32[]{:S(2)}, u32[]{:S(2)}) async-start(bf16[16,40,2048]{2,1,0:T(8,128)(2,1)} %bitcast.12), calls=%async_computation | async-start | bytes 5242880 | tf_op jit(solution)/shard_map/all_to_all | solution.py:80
  38.5 0.6 collective-permute-start.5
  39.1 0.4 collective-permute-start.6
  39.6 5.1 %collective-permute-done.5 = bf16[2048,768]{1,0:T(8,128)(2,1)} collective-permute-done((bf16[2048,768]{1,0:T(8,128)(2,1)}, bf16[2048,768]{1,0:T(8,128)(2,1)}, u32[]{:S(2)}, u32[]{:S(2)}) %collective-permute-start.5) | collective-permute-done | bytes 3145760 | tf_op jit(solution)/shard_map/ppermute | solution.py:11
  44.7 54.1 %all-to-all-done = bf16[16,40,2048]{2,1,0:T(8,128)(2,1)S(1)} async-done(((bf16[16,40,2048]{2,1,0:T(8,128)(2,1)}), bf16[16,40,2048]{2,1,0:T(8,128)(2,1)S(1)}, u32[]{:S(2)}, u32[]{:S(2)}) %all-to-all-start) | async-done | bytes 2621472 | tf_op jit(solution)/shard_map/all_to_all | solution.py:80
  98.8 5.2 %fusion.6 = f32[640,768]{1,0:T(8,128)S(1)} fusion(bf16[640,2048]{1,0:T(8,128)(2,1)S(1)} %bitcast.118, bf16[2048,768]{1,0:T(8,128)(2,1)} %collective-permute-done.5, pred[]{:T(512)S(6)} %eq.53, bf16[1,1,2048,768]{3,2,1,0:T(8,128)(2,1)} %param.11), kind=kOutput, calls=%fused_computation.14 | convolution fusion | flops 2014838784 | bytes 10878977 | tf_op jit(solution)/shard_map/cond/branch_1_fun/dot_general | solution.py:22
  104.0 4.3 %fusion.8 = f32[640,768]{1,0:T(8,128)S(1)} fusion(bf16[640,2048]{1,0:T(8,128)(2,1)S(1)} %bitcast.119, bf16[2048,768]{1,0:T(8,128)(2,1)} %collective-permute-done.4, pred[]{:T(512)S(6)} %eq.53, bf16[1,1,2048,768]{3,2,1,0:T(8,128)(2,1)S(1)} %copy-done.2), kind=kOutput, calls=%fused_computation.16 | convolution fusion | flops 2014838784 | bytes 10878977 | tf_op jit(solution)/shard_map/cond/branch_1_fun/dot_general | solution.py:21
  108.3 5.7 %convolution_convert_fusion.1 = bf16[640,2048]{1,0:T(8,128)(2,1)} fusion(bf16[768,2048]{1,0:T(8,128)(2,1)} %collective-permute-done.6, pred[]{:T(512)S(6)} %eq.53, f32[640,768]{1,0:T(8,128)S(1)} %fusion.6, f32[640,768]{1,0:T(8,128)S(1)} %fusion.8, bf16[1,1,768,2048]{3,2,1,0:T(8,128)(2,1)S(1)} %copy-done.5), kind=kOutput, calls=%fused_computation.7 | convolution fusion | flops 2019098624 | bytes 12845057 | tf_op jit(solution)/shard_map/cond/branch_1_fun/dot_general | solution.py:24
  114.1 4.7 %all-to-all-start.1 = ((bf16[16,40,2048]{2,1,0:T(8,128)(2,1)}), bf16[16,40,2048]{2,1,0:T(8,128)(2,1)S(1)}, u32[]{:S(2)}, u32[]{:S(2)}) async-start(bf16[16,40,2048]{2,1,0:T(8,128)(2,1)} %bitcast.120), calls=%async_computation.1 | async-start | bytes 5242880 | tf_op jit(solution)/shard_map/all_to_all | solution.py:81
  118.9 1.2 collective-permute-done
  120.0 0.1 copy.15
  120.1 55.3 %all-to-all-done.1 = bf16[16,40,2048]{2,1,0:T(8,128)(2,1)S(1)} async-done(((bf16[16,40,2048]{2,1,0:T(8,128)(2,1)}), bf16[16,40,2048]{2,1,0:T(8,128)(2,1)S(1)}, u32[]{:S(2)}, u32[]{:S(2)}) %all-to-all-start.1) | async-done | bytes 2621472 | tf_op jit(solution)/shard_map/all_to_all | solution.py:81
  175.4 3.3 gather_fusion
  178.7 2.3 fusion.18
  181.1 0.3 fusion.28
  181.4 0.1 fusion.30
  181.5 11.2 %scatter_custom_fusion.1 = bf16[640,2048]{1,0:T(8,128)(2,1)S(1)} fusion(s32[512]{0:T(512)S(1)} %bitcast.127, bf16[64,2048]{1,0:T(8,128)(2,1)S(1)} %fusion.30, s32[1024]{0:T(1024)S(1)} %pad_clamp_fusion.2, bf16[]{:T(256)} %constant.59.clone.1), kind=kCustom, calls=%fused_computation.28 | custom fusion | bytes 2621442 | tf_op jit(solution)/shard_map/scatter | solution.py:77
  192.7 63.1 %all_to_all.20 = bf16[16,40,2048]{2,1,0:T(8,128)(2,1)S(1)} all-to-all(bf16[16,40,2048]{2,1,0:T(8,128)(2,1)S(1)} %bitcast.117), channel_id=1, replica_groups=mesh['section'=2,'expert'=16] {'expert'}, dimensions={0} | all-to-all | bytes 5242880 | tf_op jit(solution)/shard_map/all_to_all | solution.py:80
  255.9 2.3 fusion.3
  258.2 2.3 fusion.1
  260.5 3.9 %convolution_convert_fusion = bf16[640,2048]{1,0:T(8,128)(2,1)} fusion(bf16[768,2048]{1,0:T(8,128)(2,1)} %collective-permute-done.6, pred[]{:T(512)S(6)} %eq.53, f32[640,768]{1,0:T(8,128)S(1)} %fusion.1, f32[640,768]{1,0:T(8,128)S(1)} %fusion.3, bf16[1,1,768,2048]{3,2,1,0:T(8,128)(2,1)S(1)} %copy-done.6), kind=kOutput, calls=%fused_computation.6 | convolution fusion | flops 2019098624 | bytes 12845057 | tf_op jit(solution)/shard_map/cond/branch_1_fun/dot_general | solution.py:24
  264.4 5.3 %all-to-all-start.3 = ((bf16[16,40,2048]{2,1,0:T(8,128)(2,1)}), bf16[16,40,2048]{2,1,0:T(8,128)(2,1)S(1)}, u32[]{:S(2)}, u32[]{:S(2)}) async-start(bf16[16,40,2048]{2,1,0:T(8,128)(2,1)} %bitcast.121), calls=%async_computation.3 | async-start | bytes 5242880 | tf_op jit(solution)/shard_map/all_to_all | solution.py:81
  269.6 0.1 copy.17
  269.8 58.8 %all-to-all-done.3 = bf16[16,40,2048]{2,1,0:T(8,128)(2,1)S(1)} async-done(((bf16[16,40,2048]{2,1,0:T(8,128)(2,1)}), bf16[16,40,2048]{2,1,0:T(8,128)(2,1)S(1)}, u32[]{:S(2)}, u32[]{:S(2)}) %all-to-all-start.3) | async-done | bytes 2621472 | tf_op jit(solution)/shard_map/all_to_all | solution.py:81
  328.5 3.3 gather_fusion.1
  331.8 2.3 fusion.16
  334.1 0.2 fusion.31
  334.3 3.7 %all-gather = bf16[128,2048]{1,0:T(8,128)(2,1)S(1)} all-gather(bf16[64,2048]{1,0:T(8,128)(2,1)S(1)} %fusion.31), channel_id=2, replica_groups=mesh['section'=2,'expert'=16] {'section'}, dimensions={0}, use_global_device_ids=true | all-gather | bytes 786432 | tf_op jit(solution)/shard_map/all_gather | solution.py:115
  338.0 0.8 copy.27
  (40 shorter events, 0.4 us)
Async XLA Ops:
  0.0 3.0 collective-permute-start.1
  0.7 1.7 collective-permute-start.2
  0.7 6.7 %collective-permute-start.3 = (f32[2048]{0:T(1024)}, f32[2048]{0:T(1024)S(1)}, u32[]{:S(2)}, u32[]{:S(2)}) collective-permute-start(f32[2048]{0:T(1024)} %bitcast.133), channel_id=1, source_target_pairs={{0,16},{16,0},{1,17},{17,1},{2,18},{18,2},{3,19},{19,3},{4,20},{20... | collective-permute-start | bytes 24584 | tf_op jit(solution)/shard_map/ppermute | solution.py:11
  31.9 66.9 %all-to-all-start = ((bf16[16,40,2048]{2,1,0:T(8,128)(2,1)}), bf16[16,40,2048]{2,1,0:T(8,128)(2,1)S(1)}, u32[]{:S(2)}, u32[]{:S(2)}) async-start(bf16[16,40,2048]{2,1,0:T(8,128)(2,1)} %bitcast.12), calls=%async_computation | async-start | bytes 5242880 | tf_op jit(solution)/shard_map/all_to_all | solution.py:80
  38.5 6.2 %collective-permute-start.5 = (bf16[2048,768]{1,0:T(8,128)(2,1)}, bf16[2048,768]{1,0:T(8,128)(2,1)}, u32[]{:S(2)}, u32[]{:S(2)}) collective-permute-start(bf16[2048,768]{1,0:T(8,128)(2,1)} %bitcast.139), channel_id=1, source_target_pairs={{0,16},{16,0},{1,17},{17,1},{2,18},{18,2},{3,19},{19,3},{4,20},{20... | collective-permute-start | bytes 9437192 | tf_op jit(solution)/shard_map/ppermute | solution.py:11
  39.1 64.9 %collective-permute-start.4 = (bf16[2048,768]{1,0:T(8,128)(2,1)}, bf16[2048,768]{1,0:T(8,128)(2,1)}, u32[]{:S(2)}, u32[]{:S(2)}) collective-permute-start(bf16[2048,768]{1,0:T(8,128)(2,1)} %bitcast.138), channel_id=1, source_target_pairs={{0,16},{16,0},{1,17},{17,1},{2,18},{18,2},{3,19},{19,3},{4,20},{20... | collective-permute-start | bytes 9437192 | tf_op jit(solution)/shard_map/ppermute | solution.py:11
  39.1 69.2 %collective-permute-start.6 = (bf16[768,2048]{1,0:T(8,128)(2,1)}, bf16[768,2048]{1,0:T(8,128)(2,1)}, u32[]{:S(2)}, u32[]{:S(2)}) collective-permute-start(bf16[768,2048]{1,0:T(8,128)(2,1)} %bitcast.140), channel_id=1, source_target_pairs={{0,16},{16,0},{1,17},{17,1},{2,18},{18,2},{3,19},{19,3},{4,20},{20... | collective-permute-start | bytes 9437192 | tf_op jit(solution)/shard_map/ppermute | solution.py:11
  98.8 5.2 %copy-start.2 = (bf16[1,1,2048,768]{3,2,1,0:T(8,128)(2,1)S(1)}, bf16[1,1,2048,768]{3,2,1,0:T(8,128)(2,1)}, u32[]{:S(2)}) copy-start(bf16[1,1,2048,768]{3,2,1,0:T(8,128)(2,1)} %param.10) | copy-start | bytes 9437188
  104.0 4.4 %copy-start.5 = (bf16[1,1,768,2048]{3,2,1,0:T(8,128)(2,1)S(1)}, bf16[1,1,768,2048]{3,2,1,0:T(8,128)(2,1)}, u32[]{:S(2)}) copy-start(bf16[1,1,768,2048]{3,2,1,0:T(8,128)(2,1)} %param.12) | copy-start | bytes 9437188
  114.1 4.7 %copy-start.1 = (f32[1,2,64,8]{2,3,1,0:T(8,128)S(1)}, f32[1,2,64,8]{2,3,1,0:T(8,128)}, u32[]{:S(2)}) copy-start(f32[1,2,64,8]{2,3,1,0:T(8,128)} %param.15) | copy-start | bytes 12292
  114.1 61.4 %all-to-all-start.1 = ((bf16[16,40,2048]{2,1,0:T(8,128)(2,1)}), bf16[16,40,2048]{2,1,0:T(8,128)(2,1)S(1)}, u32[]{:S(2)}, u32[]{:S(2)}) async-start(bf16[16,40,2048]{2,1,0:T(8,128)(2,1)} %bitcast.120), calls=%async_computation.1 | async-start | bytes 5242880 | tf_op jit(solution)/shard_map/all_to_all | solution.py:81
  118.8 1.2 collective-permute-start
  178.7 2.3 copy-start
  192.7 63.1 %copy-start.3 = (bf16[1,1,2048,768]{3,2,1,0:T(8,128)(2,1)S(1)}, bf16[1,1,2048,768]{3,2,1,0:T(8,128)(2,1)}, u32[]{:S(2)}) copy-start(bf16[1,1,2048,768]{3,2,1,0:T(8,128)(2,1)} %param.10) | copy-start | bytes 9437188
  255.9 2.3 copy-start.4
  258.1 2.3 copy-start.6
  264.4 64.1 %all-to-all-start.3 = ((bf16[16,40,2048]{2,1,0:T(8,128)(2,1)}), bf16[16,40,2048]{2,1,0:T(8,128)(2,1)S(1)}, u32[]{:S(2)}, u32[]{:S(2)}) async-start(bf16[16,40,2048]{2,1,0:T(8,128)(2,1)} %bitcast.121), calls=%async_computation.3 | async-start | bytes 5242880 | tf_op jit(solution)/shard_map/all_to_all | solution.py:81
where the time goes:
time: 343 us; the launch traced here: 339 us
  waiting for transfers between devices  174 us (51%)
  blocking collectives  66.8 us (19%)
  local copies, waits for them, and re-layouts  42.6 us (12%)
  matrix products  28.3 us (8%)
  starting transfers between devices  18.9 us (6%)
  other arithmetic  7.49 us (2%)
    all_to_all x2, waiting for transfers between devices, layer_step(): lax.all_to_all(run_rows(received, active, params), 'expert', split_axis=0...  114 us
    all_to_all x1, blocking collectives, layer_step(): lax.all_to_all(outgoing, 'expert', split_axis=0, concat_axis=0, tiled=True)  63.1 us
    all_to_all x1, waiting for transfers between devices, layer_step(): lax.all_to_all(outgoing, 'expert', split_axis=0, concat_axis=0, tiled=True)  54.1 us
    scatter x2, local copies, waits for them, and re-layouts, layer_step(): outgoing = jnp.zeros((groups * capacity, model_width), jnp.bfloat16).at[t...  34 us
    all_to_all x2, starting transfers between devices, layer_step(): lax.all_to_all(run_rows(received, active, params), 'expert', split_axis=0...  9.97 us
    dot_general x2, matrix products, expert_ffn(): jnp.dot(hidden_units, down_matrix, preferred_element_type=jnp.float32)  9.65 us
    dot_general x2, matrix products, expert_ffn(): up_part = jnp.dot(row_block, up_matrix, preferred_element_type=jnp.float32)  7.46 us
  transfers between devices with their start and end apart: 10, of which 5 were waited for; matrix products, arithmetic and copies ran while one was open for 5% of the time, Pallas kernels for 0%

commit v1 on v0

--- a/solution.py
+++ b/solution.py
@@ -1,6 +1,10 @@
+import functools
+
 import jax
 import jax.numpy as jnp
 from jax import lax
+from jax.experimental import pallas as pl
+from jax.experimental.pallas import tpu as pltpu
 from jax.sharding import PartitionSpec as P
 
 EPSILON = 1e-06
@@ -26,7 +30,7 @@
     )
 
 
-def local(
+def routed_local(
     tokens, norm_gain, gate_weight, up_weight, down_weight, expert_place, expert_ids, route_weights
 ):
     sections = lax.axis_size("section")
@@ -115,6 +119,291 @@
     return lax.all_gather(jnp.stack(own_finals), "section", axis=0, tiled=True)
 
 
+def layer_kernel(
+    layer,
+    depth,
+    normed_ref,
+    hidden_ref,
+    share_ref,
+    gate_hbm,
+    up_hbm,
+    down_hbm,
+    out_ref,
+    gate_mat,
+    up_mat,
+    down_mat,
+    held,
+    parts,
+    from_x_half,
+    from_y_half,
+    from_x,
+    from_y,
+    from_z,
+    sends,
+    arrivals,
+    mat_sends,
+    mat_arrivals,
+):
+    section = lax.axis_index("section")
+    me = lax.axis_index("expert")
+    level = me // 4
+    plane = lax.rem(me, 4)
+    beside_x = level * 4 + plane + 1 - 2 * lax.rem(plane, 2)
+    beside_y = level * 4 + lax.rem(plane + 2, 4)
+    rows = normed_ref.shape[0]
+    half = rows // 2
+
+    def at_level(offset):
+        return lax.rem(level + offset + depth, depth) * 4 + plane
+
+    barrier = pltpu.get_barrier_semaphore()
+    partners = [{"expert": beside_x}, {"expert": beside_y}, {"section": 1 - section}]
+    partners += [{"expert": at_level(k)} for k in range(1, depth)]
+    for partner in partners:
+        pl.semaphore_signal(
+            barrier, inc=1, device_id=partner, device_id_type=pl.DeviceIdType.MESH
+        )
+    pl.semaphore_wait(barrier, len(partners))
+
+    started = []
+
+    def send(kind, k, source, target, peer):
+        copy = pltpu.make_async_remote_copy(
+            src_ref=source,
+            dst_ref=target,
+            send_sem=sends.at[kind, k],
+            recv_sem=arrivals.at[kind, k],
+            device_id={"expert": peer},
+            device_id_type=pl.DeviceIdType.MESH,
+        )
+        copy.start()
+        started.append(copy)
+        return copy
+
+    lower, upper = pl.ds(0, half), pl.ds(half, rows - half)
+
+    by_z = [None] + [
+        send(0, k, normed_ref, held.at[k, 0], at_level(k)) for k in range(1, depth)
+    ]
+    by_x = {0: send(1, 0, normed_ref, held.at[0, 1], beside_x)}
+    by_y = {0: send(2, 0, normed_ref, held.at[0, 2], beside_y)}
+
+    mats = [(gate_hbm, gate_mat), (up_hbm, up_mat), (down_hbm, down_mat)]
+    remote_mats = [
+        pltpu.make_async_remote_copy(
+            src_ref=source,
+            dst_ref=target,
+            send_sem=mat_sends.at[i],
+            recv_sem=mat_arrivals.at[i],
+            device_id={"section": 1 - section},
+            device_id_type=pl.DeviceIdType.MESH,
+        )
+        for i, (source, target) in enumerate(mats)
+    ]
+    local_mats = [
+        pltpu.make_async_copy(source, target, mat_sends.at[3 + i])
+        for i, (source, target) in enumerate(mats)
+    ]
+
+    @pl.when(section == layer)
+    def _():
+        for copy in remote_mats + local_mats:
+            copy.start()
+
+    held[0, 0] = normed_ref[...]
+
+    by_xy, by_yx = {}, {}
+
+    def relay(k):
+        by_z[k].wait_recv()
+        by_x[k] = send(1, k, held.at[k, 0], held.at[k, 1], beside_x)
+        by_y[k] = send(2, k, held.at[k, 0], held.at[k, 2], beside_y)
+
+    def relay_diagonal(k):
+        by_x[k].wait_recv()
+        by_xy[k] = send(3, k, held.at[k, 1, lower], held.at[k, 3, lower], beside_y)
+        by_y[k].wait_recv()
+        by_yx[k] = send(4, k, held.at[k, 2, upper], held.at[k, 3, upper], beside_x)
+
+    halves_y, halves_x, fulls_x, fulls_y, backs = {}, {}, {}, {}, {}
+
+    def compute(k):
+        by_xy[k].wait_recv()
+        by_yx[k].wait_recv()
+        block = held[k].reshape(4 * rows, held.shape[3])
+        gate_part = jnp.dot(block, gate_mat[...], preferred_element_type=jnp.float32)
+        up_part = jnp.dot(block, up_mat[...], preferred_element_type=jnp.float32)
+        hidden_units = (gate_part / (1.0 + jnp.exp(-gate_part)) * up_part).astype(jnp.bfloat16)
+        out = jnp.dot(hidden_units, down_mat[...], preferred_element_type=jnp.float32)
+        out = out.astype(jnp.bfloat16).astype(jnp.float32) * share_ref[k]
+        parts[k] = out.astype(jnp.bfloat16).reshape(parts.shape[1:])
+        halves_y[k] = send(5, k, parts.at[k, 3, lower], from_y_half.at[k], beside_y)
+        halves_x[k] = send(6, k, parts.at[k, 3, upper], from_x_half.at[k], beside_x)
+
+    def add(*terms):
+        total = terms[0].astype(jnp.float32)
+        for term in terms[1:]:
+            total = total + term.astype(jnp.float32)
+        return total
+
+    def combine_half(k):
+        halves_y[k].wait_recv()
+        parts[k, 1, lower] = add(parts[k, 1, lower], from_y_half[k]).astype(jnp.bfloat16)
+        fulls_x[k] = send(7, k, parts.at[k, 1], from_x.at[k], beside_x)
+        halves_x[k].wait_recv()
+        parts[k, 2, upper] = add(parts[k, 2, upper], from_x_half[k]).astype(jnp.bfloat16)
+        fulls_y[k] = send(8, k, parts.at[k, 2], from_y.at[k], beside_y)
+
+    def combine_full(k):
+        fulls_x[k].wait_recv()
+        fulls_y[k].wait_recv()
+        parts[k, 0] = add(parts[k, 0], from_x[k], from_y[k]).astype(jnp.bfloat16)
+        backs[k] = send(9, k, parts.at[k, 0], from_z.at[k], at_level(-k))
+
+    def wait_mats():
+        @pl.when(section == layer)
+        def _():
+            for copy in remote_mats:
+                copy.wait_send()
+            for copy in local_mats:
+                copy.wait()
+
+        @pl.when(section != layer)
+        def _():
+            for copy in remote_mats:
+                copy.wait_recv()
+
+    relay(1)
+    relay_diagonal(0)
+    for k in range(depth):
+        if k + 2 < depth:
+            relay(k + 2)
+        if k + 1 < depth:
+            relay_diagonal(k + 1)
+        if k == 0:
+            wait_mats()
+        compute(k)
+        if k >= 1:
+            combine_half(k - 1)
+        if k >= 2:
+            if k > 2:
+                combine_full(k - 2)
+    combine_half(depth - 1)
+    for k in range(max(1, depth - 2), depth):
+        combine_full(k)
+    fulls_x[0].wait_recv()
+    fulls_y[0].wait_recv()
+    mixture = add(parts[0, 0], from_x[0], from_y[0])
+    for k in range(1, depth):
+        backs[k].wait_recv()
+        mixture = mixture + from_z[k].astype(jnp.float32)
+    out_ref[...] = (hidden_ref[...].astype(jnp.float32) + mixture).astype(jnp.bfloat16)
+    for copy in started:
+        copy.wait_send()
+
+
+def layer_call(layer, depth, normed, hidden, share, gate_matrix, up_matrix, down_matrix):
+    rows, width = normed.shape
+    vmem = pl.BlockSpec(memory_space=pltpu.VMEM)
+    anywhere = pl.BlockSpec(memory_space=pl.ANY)
+    bf16 = jnp.bfloat16
+    return pl.pallas_call(
+        functools.partial(layer_kernel, layer, depth),
+        out_shape=jax.ShapeDtypeStruct((rows, width), bf16),
+        in_specs=[vmem, vmem, vmem, anywhere, anywhere, anywhere],
+        out_specs=vmem,
+        scratch_shapes=[
+            pltpu.VMEM(gate_matrix.shape, bf16),
+            pltpu.VMEM(up_matrix.shape, bf16),
+            pltpu.VMEM(down_matrix.shape, bf16),
+            pltpu.VMEM((depth, 4, rows, width), bf16),
+            pltpu.VMEM((depth, 4, rows, width), bf16),
+            pltpu.VMEM((depth, rows // 2, width), bf16),
+            pltpu.VMEM((depth, rows // 2, width), bf16),
+            pltpu.VMEM((depth, rows, width), bf16),
+            pltpu.VMEM((depth, rows, width), bf16),
+            pltpu.VMEM((depth, rows, width), bf16),
+            pltpu.SemaphoreType.DMA((10, depth)),
+            pltpu.SemaphoreType.DMA((10, depth)),
+            pltpu.SemaphoreType.DMA((6,)),
+            pltpu.SemaphoreType.DMA((3,)),
+        ],
+        compiler_params=pltpu.CompilerParams(
+            collective_id=layer,
+            has_side_effects=True,
+            vmem_limit_bytes=56 * 1024 * 1024,
+        ),
+    )(normed, hidden, share, gate_matrix, up_matrix, down_matrix)
+
+
+def dense_local(
+    tokens, norm_gain, gate_weight, up_weight, down_weight, expert_place, expert_ids, route_weights
+):
+    groups = lax.axis_size("expert")
+    section_index = lax.axis_index("section")
+    expert_index = lax.axis_index("expert")
+    is_first = section_index == 0
+    lanes = jnp.arange(groups, dtype=jnp.int32)
+    held_by = jnp.sum(
+        jnp.where(expert_ids[0][..., None] == lanes, expert_place[0], 0), axis=-1
+    )
+    dense = jnp.sum(
+        jnp.where(held_by[..., None] == lanes, route_weights[0][..., None], 0.0), axis=2
+    )
+    kept = jnp.where(is_first, dense[0], dense[1])
+    sent = jnp.where(is_first, dense[1], dense[0])
+    swapped = from_behind(sent, "section", 1)
+    both = jnp.stack([jnp.where(is_first, kept, swapped), jnp.where(is_first, swapped, kept)])
+    shares = lax.all_gather(both, "expert", axis=1, tiled=True)
+    shares = lax.dynamic_index_in_dim(shares, expert_index, 2, keepdims=True)
+
+    other_gain = from_behind(norm_gain[0], "section", 1)
+    gains = (
+        jnp.where(is_first, norm_gain[0], other_gain),
+        jnp.where(is_first, other_gain, norm_gain[0]),
+    )
+    depth = groups // 4
+    plane = lax.rem(expert_index, 4)
+    steps = jnp.arange(depth, dtype=jnp.int32)[:, None]
+    columns = jnp.bitwise_xor(plane, jnp.arange(4, dtype=jnp.int32))[None, :]
+    origin = (lax.rem(expert_index // 4 - steps + depth, depth) * 4 + columns).reshape(-1)
+    rows = tokens.shape[1]
+    shares = shares.reshape(2, groups, rows)[:, origin].reshape(2, depth, 4 * rows, 1)
+
+    hidden = lax.dynamic_index_in_dim(tokens, section_index, 0, keepdims=False)
+    for layer in range(2):
+        normed = normalize(hidden, gains[layer])
+        hidden = layer_call(
+            layer,
+            depth,
+            normed,
+            hidden,
+            shares[layer],
+            gate_weight[0, 0],
+            up_weight[0, 0],
+            down_weight[0, 0],
+        )
+    return lax.all_gather(hidden[None], "section", axis=0, tiled=True)
+
+
+def local(
+    tokens, norm_gain, gate_weight, up_weight, down_weight, expert_place, expert_ids, route_weights
+):
+    dense = 2 * expert_ids.shape[3] >= expert_place.shape[1] and tokens.shape[0] == 2
+    dense = dense and lax.axis_size("expert") % 4 == 0 and lax.axis_size("expert") > 4
+    run = dense_local if dense else routed_local
+    return run(
+        tokens,
+        norm_gain,
+        gate_weight,
+        up_weight,
+        down_weight,
+        expert_place,
+        expert_ids,
+        route_weights,
+    )
+
+
 def solution(mesh):
     in_specs = (
         P(None, "expert", None),

time: 343 us -> 239 us (0.70)
  the two profiles are of different devices: /device:TPU:15 before, /device:TPU:0 now
where the time goes in v1:
time: 239 us
  Pallas kernels  174 us (73%)
  blocking collectives  51.5 us (22%)
  other arithmetic  6.52 us (3%)
  local copies, waits for them, and re-layouts  5.85 us (2%)
    pallas_call x2, Pallas kernels, layer_call(): pl.pallas_call(functools.partial(layer_kernel, layer, depth), out_shape=j...  174 us
    all_gather x1, blocking collectives, dense_local(): shares = lax.all_gather(both, 'expert', axis=1, tiled=True)  49.1 us
  transfers between devices with their start and end apart: 2, of which 0 were waited for; matrix products, arithmetic and copies ran while one was open for 3% of the time, Pallas kernels for 0%

profile of v1, /device:TPU:0, one launch (start us, length us, event | category | flops | bytes accessed | tf_op | source)
XLA Modules:
  0.0 239.1 jit_solution(7522825756504342294)
XLA Ops:
  0.0 0.0 copy-start.1
  0.0 0.8 select_reduce_fusion.1
  0.8 0.7 select_reduce_fusion
  1.6 0.6 collective-permute-start.1
  2.1 0.1 collective-permute-start
  2.2 0.1 broadcast_add_fusion
  2.3 0.1 add.74
  2.4 1.1 fusion
  3.5 0.0 copy-start
  3.5 0.0 collective-permute-done.1
  3.6 0.1 copy.31
  3.7 49.1 %all_gather.6 = f32[2,1024,16]{2,0,1:T(2,128)S(1)} all-gather(f32[2,64,16]{2,0,1:T(2,128)S(1)} %copy.31), channel_id=1, replica_groups=mesh['section'=2,'expert'=16] {'expert'}, dimensions={1}, use_global_device_ids=true | all-gather | bytes 139264 | tf_op jit(solution)/shard_map/all_gather | solution.py:357
  52.7 1.1 constant_dynamic-slice_fusion
  53.9 0.5 copy.32
  54.3 0.1 reshape.88
  54.5 0.6 gather_fusion
  55.1 1.3 squeeze.42.share_ref
  56.4 1.3 squeeze.43.share_ref
  57.6 0.0 collective-permute-done
  57.6 0.0 copy-done.1
  57.6 0.8 fusion.2.normed_ref
  58.5 0.0 copy-done
  58.5 80.6 %shard_map.82.hidden_ref = bf16[64,2048]{1,0:T(8,128)(2,1)} custom-call(bf16[64,2048]{1,0:T(8,128)(2,1)} %fusion.2.normed_ref, bf16[64,2048]{1,0:T(8,128)(2,1)} %copy-done, f32[4,256,1]{2,1,0:T(8,128)} %squeeze.42.share_ref, bf16[2048,768]{1,0:T(8,128)(2,1)} %bitcast.29, bf16[2048,768]{1,0:T(8,128)(2,1)} %bitcast.31, bf16[768,2048]{1,0:T(8,128)(2,1)} %bitcast.33), custom_call_target="tpu_custom_call" | custom-call | tf_op jit(solution)/shard_map/pallas_call | solution.py:310
  139.1 1.1 fusion.3
  140.3 1.8 fusion.5.normed_ref
  142.0 93.9 %shard_map.83 = bf16[64,2048]{1,0:T(8,128)(2,1)} custom-call(bf16[64,2048]{1,0:T(8,128)(2,1)} %fusion.5.normed_ref, bf16[64,2048]{1,0:T(8,128)(2,1)} %shard_map.82.hidden_ref, f32[4,256,1]{2,1,0:T(8,128)} %squeeze.43.share_ref, bf16[2048,768]{1,0:T(8,128)(2,1)} %bitcast.30, bf16[2048,768]{1,0:T(8,128)(2,1)} %bitcast.32, bf16[768,2048]{1,0:T(8,128)(2,1)} %bitcast.34), custom_call_target="tpu_custom_call" | custom-call | tf_op jit(solution)/shard_map/pallas_call | solution.py:310
  235.9 2.4 %all-gather = bf16[128,2048]{1,0:T(8,128)(2,1)S(1)} all-gather(bf16[64,2048]{1,0:T(8,128)(2,1)} %shard_map.83), channel_id=2, replica_groups=mesh['section'=2,'expert'=16] {'section'}, dimensions={0}, use_global_device_ids=true | all-gather | bytes 786432 | tf_op jit(solution)/shard_map/all_gather | solution.py:386
  238.3 0.8 copy.37
  (11 shorter events, 0.1 us)
Async XLA Ops:
  0.0 57.6 %copy-start.1 = (f32[1,2048]{1,0:T(1,128)S(1)}, f32[1,2048]{1,0:T(1,128)}, u32[]{:S(2)}) copy-start(f32[1,2048]{1,0:T(1,128)} %param.9) | copy-start | bytes 24580
  1.6 2.0 collective-permute-start.1
  2.1 55.5 %collective-permute-start = (f32[2048]{0:T(1024)}, f32[2048]{0:T(1024)S(1)}, u32[]{:S(2)}, u32[]{:S(2)}) collective-permute-start(f32[2048]{0:T(1024)} %bitcast.39), channel_id=1, source_target_pairs={{0,16},{16,0},{1,17},{17,1},{2,18},{18,2},{3,19},{19,3},{4,20},{20... | collective-permute-start | bytes 24584 | tf_op jit(solution)/shard_map/ppermute | solution.py:15
  3.5 55.0 %copy-start = (bf16[64,2048]{1,0:T(8,128)(2,1)}, bf16[64,2048]{1,0:T(8,128)(2,1)S(1)}, u32[]{:S(2)}) copy-start(bf16[64,2048]{1,0:T(8,128)(2,1)S(1)} %get-tuple-element.8.hidden_ref) | copy-start | bytes 786436
